TPU v7x, 128 devices: a whole 4x4x4 slice. The times are simulated.
128 devices in a mesh: seq: 16 (over z, x), exp: 8 (over y, core).
Axes of the slice: x: 4, y: 4, z: 4, core: 2. Of those that a mesh axis runs over, the one named last changes fastest.
Arguments:
- tokens: bfloat16 [8, 2048, 4096], P('exp', 'seq'), may hold values from -6 to 6
- out_grad: bfloat16 [8, 2048, 4096], P('exp', 'seq'), may hold values from -0.59765625 to 0.59765625
- router_weight: bfloat16 [4096, 128], replicated, may hold values from -8 to 8
- gate_weight: bfloat16 [128, 4096, 768], P(('seq', 'exp')), may hold values from -0.09375 to 0.09375
- up_weight: bfloat16 [128, 4096, 768], P(('seq', 'exp')), may hold values from -0.09375 to 0.09375
- down_weight: bfloat16 [128, 768, 4096], P(('seq', 'exp')), may hold values from -0.21875 to 0.21875
- saved_gate: bfloat16 [128, 2048, 768], P(('seq', 'exp')), may hold values from -6 to 6
- saved_up: bfloat16 [128, 2048, 768], P(('seq', 'exp')), may hold values from -6 to 6
- expert_ids: int32 [8, 2048, 8], P('exp', 'seq'), may hold values from 0 to 127, as said below
- aux_weight: float32 [1], replicated, may hold values from 2 to 6
Outputs:
- token_grad: bfloat16 [8, 2048, 4096], P('exp', 'seq')
- combine_grad: float32 [8, 2048, 8], P('exp', 'seq')
- router_grad: float32 [4096, 128], P(('seq', 'exp'))
Inputs may be any that keep to these rules, and one draw needn't show every extreme that they name: `expert_ids`: among the rows of one device (128 tokens) each expert is named at most 16 times, and some expert exactly 16 times; a token's 8 experts differ.
All inputs are finite; a program needn't handle non-finite values.
Results may differ from a plain program's by a relative error of at most 0.013.
Values may be sent and summed in bfloat16 or wider, within the bound.
A program may use at most 192 MiB of HBM per device.

v0:
```python
import functools
import jax
import jax.numpy as jnp
from jax import lax
from jax.sharding import Mesh
from jax.sharding import PartitionSpec as P

SEQ = ("seq_0", "seq_1")
EXP = ("exp_0", "exp_1")
SEQ_EXP = ("seq_0", "seq_1", "exp_0", "exp_1")


def over_axes(shard, axes):
    return functools.reduce(lax.psum, axes, shard)


def in_blocks(shard, dim, size):
    shape = shard.shape
    parts = shard.reshape(*shape[:dim], size, shape[dim] // size, *shape[dim + 1 :])
    return jnp.moveaxis(parts, dim, 0)


def summed_on_arrival(shard, axis, dim):
    size = lax.axis_size(axis)
    parts = lax.all_to_all(in_blocks(shard, dim, size), axis, 0, 0, tiled=True)
    return jnp.sum(parts, axis=0)


def summed_rows(shard, axes, dim):
    far, near = axes
    own = summed_on_arrival(in_blocks(shard, dim, lax.axis_size(far)), near, dim + 1)
    return jnp.sum(lax.all_to_all(own, far, 0, 0, tiled=True), axis=0)


def filled_up(lines, size):
    spare = -len(lines) % size
    return jnp.pad(lines, [(0, spare)] + [(0, 0)] * (lines.ndim - 1))


def from_everyone(shard, axis):
    size = lax.axis_size(axis)
    return lax.all_to_all(
        jnp.broadcast_to(shard[None], (size, *shard.shape)), axis, 0, 0, tiled=True
    )


def laid_out(parts, dim):
    shape = list(parts.shape[1:])
    shape[dim] *= parts.shape[0]
    return jnp.moveaxis(parts, 0, dim).reshape(shape)


def gathered_by_axis(shard, axes, dim):
    far, near = axes
    parts = from_everyone(from_everyone(shard, far), near)
    return laid_out(parts.swapaxes(0, 1).reshape(-1, *shard.shape), dim)


def total_of(shard, axes):
    lines = shard.reshape(-1, shard.shape[-1])
    own = summed_rows(filled_up(lines, lax.axis_size(axes[0]) * lax.axis_size(axes[1])), axes, 0)
    whole = gathered_by_axis(own, axes, 0)
    return whole[: len(lines)].reshape(shard.shape)


def expert_backward(grad_rows, gate_rows, w_gate, w_up, w_down, pre_gate, pre_up):
    upstream = jnp.einsum("rd,fd->rf", grad_rows, w_down, preferred_element_type=jnp.float32)
    first = pre_gate.astype(jnp.float32)
    second = pre_up.astype(jnp.float32)
    gate_sig = jax.nn.sigmoid(first)
    gate_act = first * gate_sig
    hidden = gate_act * second
    slot_combine = jnp.sum(upstream * hidden, axis=-1).astype(jnp.bfloat16)
    scaled = gate_rows.astype(jnp.float32)[:, None] * upstream
    grad_first = (scaled * second * gate_sig * (1.0 + first * (1.0 - gate_sig))).astype(
        jnp.bfloat16
    )
    grad_second = (scaled * gate_act).astype(jnp.bfloat16)
    back_rows = jnp.einsum("rf,df->rd", grad_first, w_gate, preferred_element_type=jnp.float32)
    back_rows = back_rows + jnp.einsum(
        "rf,df->rd", grad_second, w_up, preferred_element_type=jnp.float32
    )
    return (back_rows.astype(jnp.bfloat16), slot_combine)


def shards(
    tokens,
    out_grad,
    router_weight,
    gate_weight,
    up_weight,
    down_weight,
    saved_gate,
    saved_up,
    expert_ids,
    aux_weight,
):
    seq_size = lax.axis_size(SEQ)
    exp_size = lax.axis_size(EXP)
    devices = seq_size * exp_size
    inputs = tokens[0]
    upstream_grad = out_grad[0]
    chosen_ids = expert_ids[0]
    tok_rows, top_count = chosen_ids.shape
    model_width = inputs.shape[1]
    experts = router_weight.shape[1]
    capacity = saved_gate.shape[1] // devices
    logits = jnp.dot(inputs, router_weight, preferred_element_type=jnp.float32)
    router_probs = jax.nn.softmax(logits, axis=-1)
    chosen = jnp.take_along_axis(router_probs, chosen_ids, axis=1)
    chosen_sum = jnp.sum(chosen, axis=1, keepdims=True)
    gate_vals = chosen / chosen_sum
    onehot = (
        chosen_ids.reshape(-1)[:, None] == jnp.arange(experts, dtype=jnp.int32)[None, :]
    ).astype(jnp.int32)
    rank_before = jnp.cumsum(onehot, axis=0) - onehot
    slot_pos = jnp.sum(rank_before * onehot, axis=1)
    slot_index = chosen_ids.reshape(-1) * capacity + slot_pos
    token_order = jnp.arange(tok_rows * top_count, dtype=jnp.int32) // top_count
    slot_token = (
        jnp.full((experts * capacity,), tok_rows, jnp.int32).at[slot_index].set(token_order)
    )
    grad_padded = jnp.concatenate(
        [upstream_grad, jnp.zeros((1, model_width), jnp.bfloat16)], axis=0
    )
    grad_slots = grad_padded[slot_token]
    gate_slots = (
        jnp.zeros((experts * capacity,), jnp.bfloat16)
        .at[slot_index]
        .set(gate_vals.reshape(-1).astype(jnp.bfloat16))
    )
    chosen_count = jnp.sum(onehot.reshape(tok_rows, top_count, experts), axis=1).astype(jnp.float32)
    local_counts = jnp.sum(chosen_count, axis=0)
    seq_counts = over_axes(local_counts, SEQ)
    recv_grad, recv_gate = (
        lax.all_to_all(
            grad_slots.reshape(experts, 1, capacity, model_width),
            SEQ_EXP,
            split_axis=0,
            concat_axis=1,
            tiled=True,
        ),
        lax.all_to_all(
            gate_slots.reshape(experts, 1, capacity),
            SEQ_EXP,
            split_axis=0,
            concat_axis=1,
            tiled=True,
        ),
    )
    back_rows, slot_combine = expert_backward(
        recv_grad.reshape(-1, model_width),
        recv_gate.reshape(-1),
        gate_weight[0],
        up_weight[0],
        down_weight[0],
        saved_gate[0],
        saved_up[0],
    )
    returned, combine_back = (
        lax.all_to_all(
            back_rows.reshape(1, devices, capacity, model_width),
            SEQ_EXP,
            split_axis=1,
            concat_axis=0,
            tiled=True,
        ),
        lax.all_to_all(
            slot_combine.reshape(1, devices, capacity),
            SEQ_EXP,
            split_axis=1,
            concat_axis=0,
            tiled=True,
        ),
    )
    returned_rows = returned.reshape(experts * capacity, model_width)
    expert_sum = jnp.sum(
        returned_rows[slot_index].reshape(tok_rows, top_count, model_width).astype(jnp.float32),
        axis=1,
    )
    combine_grad = (
        combine_back.reshape(-1)[slot_index].reshape(tok_rows, top_count).astype(jnp.float32)
    )
    prob_sel = (
        combine_grad - jnp.sum(gate_vals * combine_grad, axis=1, keepdims=True)
    ) / chosen_sum
    prob_grad = jnp.einsum(
        "tk,tke->te", prob_sel, onehot.reshape(tok_rows, top_count, experts).astype(jnp.float32)
    )
    fraction = experts * seq_counts / (top_count * tok_rows * seq_size)
    prob_grad = prob_grad + aux_weight[0] * fraction[None, :]
    dlogits = router_probs * (prob_grad - jnp.sum(router_probs * prob_grad, axis=1, keepdims=True))
    logit_grad = dlogits.astype(jnp.bfloat16)
    token_grad = expert_sum + jnp.einsum(
        "te,de->td", logit_grad, router_weight, preferred_element_type=jnp.float32
    )
    own_rows = model_width // devices
    router_full = total_of(
        jnp.einsum("td,te->de", inputs, logit_grad, preferred_element_type=jnp.float32),
        (("seq_0", "seq_1", "exp_0"), "exp_1"),
    )
    router_grad = lax.dynamic_slice_in_dim(
        router_full, lax.axis_index(SEQ_EXP) * own_rows, own_rows, 0
    )
    return (token_grad.astype(jnp.bfloat16)[None], combine_grad[None], router_grad)


def solution(mesh):
    torus = Mesh(mesh.devices.reshape(4, 4, 4, 2), ("seq_0", "seq_1", "exp_0", "exp_1"))
    return jax.shard_map(
        shards,
        mesh=torus,
        in_specs=(
            P(EXP, SEQ, None),
            P(EXP, SEQ, None),
            P(),
            P(SEQ_EXP, None, None),
            P(SEQ_EXP, None, None),
            P(SEQ_EXP, None, None),
            P(SEQ_EXP, None, None),
            P(SEQ_EXP, None, None),
            P(EXP, SEQ, None),
            P(),
        ),
        out_specs=(P(EXP, SEQ, None), P(EXP, SEQ, None), P(SEQ_EXP, None)),
        check_vma=False,
    )
```

profile of v0, /device:TPU:82, one launch (start us, length us, event | category | flops | bytes accessed | tf_op | source)
XLA Modules:
  0.0 671.6 jit_solution(18006657790768191358)
XLA Ops:
  0.6 0.9 copy.61
  3.5 4.3 scatter_custom_fusion.1
  7.8 1.3 concatenate.3
  9.2 14.3 %gather_fusion = bf16[2048,4096]{1,0:T(8,128)(2,1)} fusion(bf16[129,4096]{1,0:T(8,128)(2,1)S(1)} %concatenate.3, s32[2048]{0:T(1024)S(1)} %fusion.34), kind=kCustom, calls=%fused_computation | custom fusion | bytes 33562624 | tf_op jit(solution)/shard_map/gather | solution.py:126
  23.5 10.4 %all-to-all-start.1 = ((bf16[128,1,16,4096]{3,2,1,0:T(8,128)(2,1)}), bf16[128,1,16,4096]{3,2,1,0:T(8,128)(2,1)}, u32[]{:S(2)}, u32[]{:S(2)}) async-start(bf16[128,1,16,4096]{3,2,1,0:T(8,128)(2,1)} %bitcast.94), calls=%async_computation.1 | async-start | bytes 33554432 | tf_op jit(solution)/shard_map/all_to_all | solution.py:136
  33.9 4.8 copy.70
  38.7 4.7 copy.69
  44.3 7.0 %gather_fusion.3 = f32[1024]{0:T(1024)S(1)} fusion(f32[128,128]{0,1:T(8,128)S(1)} %fusion.32, s32[1024]{0:T(1024)S(1)} %reshape.225), kind=kCustom, calls=%fused_computation.3 | custom fusion | bytes 16384 | tf_op jit(solution)/shard_map/jit(take_along_axis)/gather | solution.py:110
  52.4 7.6 %scatter_custom_fusion = bf16[2048]{0:T(1024)(128)(2,1)S(1)} fusion(s32[1024]{0:T(1024)S(1)} %bitcast.104, bf16[1024]{0:T(1024)(128)(2,1)S(1)} %divide_convert_fusion, bf16[]{:T(256)} %constant.29.clone.1), kind=kCustom, calls=%fused_computation.88 | custom fusion | bytes 4098 | tf_op jit(solution)/shard_map/scatter | solution.py:130
  61.0 116.0 %psum.14 = f32[128]{0:T(128)S(1)} all-reduce(f32[128]{0:T(128)S(1)} %convert_reduce_fusion.3), channel_id=1, replica_groups=mesh['seq_0'=4,'seq_1'=4,'exp_0'=4,'exp_1'=2] {'seq_0'}, use_global_device_ids=true, to_apply=%region_13.14 | all-reduce | flops 128 | bytes 1024 | tf_op jit(solution)/shard_map/psum | solution.py:14
  177.0 62.2 %psum.15 = f32[128]{0:T(128)S(1)} all-reduce(f32[128]{0:T(128)S(1)} %psum.14), channel_id=1, replica_groups=mesh['seq_0'=4,'seq_1'=4,'exp_0'=4,'exp_1'=2] {'seq_1'}, use_global_device_ids=true, to_apply=%region_14.15 | all-reduce | flops 128 | bytes 1024 | tf_op jit(solution)/shard_map/psum | solution.py:14
  239.2 8.9 %all-to-all-done.1 = bf16[128,1,16,4096]{3,2,1,0:T(8,128)(2,1)} async-done(((bf16[128,1,16,4096]{3,2,1,0:T(8,128)(2,1)}), bf16[128,1,16,4096]{3,2,1,0:T(8,128)(2,1)}, u32[]{:S(2)}, u32[]{:S(2)}) %all-to-all-start.1) | async-done | bytes 16777248 | tf_op jit(solution)/shard_map/all_to_all | solution.py:136
  248.0 15.1 %all-to-all-start = ((bf16[128,1,16]{2,1,0:T(2,128)(2,1)}), bf16[128,1,16]{2,1,0:T(2,128)(2,1)S(1)}, u32[]{:S(2)}, u32[]{:S(2)}) async-start(bf16[128,1,16]{2,1,0:T(2,128)(2,1)} %reshape.251), calls=%async_computation | async-start | bytes 131072 | tf_op jit(solution)/shard_map/all_to_all | solution.py:143
  263.1 22.5 %fusion.4 = (bf16[2048]{0:T(1024)(128)(2,1)S(1)}, f32[2048,768]{0,1:T(8,128)}) fusion(bf16[1,2048,768]{1,2,0:T(8,128)(2,1)} %copy.69, bf16[1,2048,768]{1,2,0:T(8,128)(2,1)} %copy.70, bf16[2048,4096]{1,0:T(8,128)(2,1)} %bitcast.11, bf16[1,768,4096]{2,1,0:T(8,128)(2,1)} %param.15), kind=kOutput, calls=%fused_computation.17 | convolution fusion | flops 12899055616 | bytes 35655680 | tf_op jit(solution)/shard_map/rd,fd->rf/dot_general | solution.py:67
  286.4 9.8 %all-to-all-start.3 = ((bf16[1,128,16]{2,0,1:T(2,128)(2,1)}), bf16[1,128,16]{2,0,1:T(2,128)(2,1)S(1)}, u32[]{:S(2)}, u32[]{:S(2)}) async-start(bf16[1,128,16]{2,0,1:T(2,128)(2,1)} %convert_element_type.124), calls=%async_computation.3 | async-start | bytes 131072 | tf_op jit(solution)/shard_map/all_to_all | solution.py:168
  296.5 4.9 all-to-all-done.3
  301.6 6.8 %gather_fusion.2 = bf16[1024]{0:T(1024)(128)(2,1)S(1)} fusion(bf16[2048]{0:T(1024)(128)(2,1)S(1)} %reshape.194, s32[1024]{0:T(1024)S(1)} %broadcast_clamp_fusion), kind=kCustom, calls=%fused_computation.2 | custom fusion | bytes 8192 | tf_op jit(solution)/shard_map/gather | solution.py:182
  309.5 1.8 convolution_bitcast_fusion
  311.3 1.9 copy.73
  313.4 5.4 all_to_all.56
  318.8 1.2 reduce_sum.111
  320.0 9.7 %all-to-all-start.5 = ((f32[64,32,128]{2,1,0:T(8,128)}), f32[64,32,128]{2,1,0:T(8,128)S(1)}, u32[]{:S(2)}, u32[]{:S(2)}) async-start(f32[64,32,128]{2,1,0:T(8,128)} %reduce_sum.111), calls=%async_computation.5 | async-start | bytes 2097152 | tf_op jit(solution)/shard_map/all_to_all | solution.py:32
  329.7 29.5 %fusion.10 = f32[2048,4096]{1,0:T(8,128)} fusion(bf16[1,4096,768]{2,1,0:T(8,128)(2,1)} %param.13, f32[2048,768]{0,1:T(8,128)} %get-tuple-element.18, bf16[1,2048,768]{1,2,0:T(8,128)(2,1)} %copy.69, bf16[1,2048,768]{1,2,0:T(8,128)(2,1)} %copy.70, f32[2048]{0:T(1024)S(1)} %reshape.195), kind=kOutput, calls=%fused_computation.23 | convolution fusion | flops 12905349120 | bytes 52436992 | tf_op jit(solution)/shard_map/rf,df->rd/dot_general | solution.py:79
  359.4 1.1 broadcast_in_dim.24
  360.5 10.3 %all-to-all-start.6 = ((f32[64,32,128]{2,1,0:T(8,128)}), f32[64,32,128]{2,1,0:T(8,128)S(1)}, u32[]{:S(2)}, u32[]{:S(2)}) async-start(f32[64,32,128]{2,1,0:T(8,128)} %broadcast_in_dim.24), calls=%async_computation.6 | async-start | bytes 2097152 | tf_op jit(solution)/shard_map/all_to_all | solution.py:42
  370.8 27.9 %add_convert_fusion = bf16[2048,4096]{1,0:T(8,128)(2,1)} fusion(f32[2048,4096]{1,0:T(8,128)} %fusion.10, bf16[1,4096,768]{2,1,0:T(8,128)(2,1)} %param.14, f32[2048,768]{0,1:T(8,128)} %get-tuple-element.18, f32[2048]{0:T(1024)S(1)} %reshape.195, bf16[1,2048,768]{1,2,0:T(8,128)(2,1)} %copy.70), kind=kOutput, calls=%fused_computation.6 | convolution fusion | flops 12914262016 | bytes 66068480 | tf_op jit(solution)/shard_map/rf,df->rd/dot_general | solution.py:80
  399.0 5.4 all_to_all.57
  404.4 10.6 %all-to-all-start.2 = ((bf16[1,128,16,4096]{3,2,0,1:T(8,128)(2,1)}), bf16[1,128,16,4096]{3,2,0,1:T(8,128)(2,1)}, u32[]{:S(2)}, u32[]{:S(2)}) async-start(bf16[1,128,16,4096]{3,2,0,1:T(8,128)(2,1)} %bitcast.95), calls=%async_computation.2 | async-start | bytes 33554432 | tf_op jit(solution)/shard_map/all_to_all | solution.py:161
  416.6 219.9 %all-to-all-done.2 = bf16[1,128,16,4096]{3,2,0,1:T(8,128)(2,1)} async-done(((bf16[1,128,16,4096]{3,2,0,1:T(8,128)(2,1)}), bf16[1,128,16,4096]{3,2,0,1:T(8,128)(2,1)}, u32[]{:S(2)}, u32[]{:S(2)}) %all-to-all-start.2) | async-done | bytes 16777248 | tf_op jit(solution)/shard_map/all_to_all | solution.py:161
  636.5 23.1 %gather_fusion.1 = bf16[1024,4096]{1,0:T(8,128)(2,1)} fusion(bf16[2048,4096]{1,0:T(8,128)(2,1)} %bitcast.20, s32[1024]{0:T(1024)S(1)} %broadcast_clamp_fusion), kind=kCustom, calls=%fused_computation.1 | custom fusion | bytes 16781312 | tf_op jit(solution)/shard_map/gather | solution.py:178
  659.6 9.1 %convert_reduce_fusion = f32[128,4096]{1,0:T(8,128)S(1)} fusion(bf16[1024,4096]{1,0:T(8,128)(2,1)} %gather_fusion.1), kind=kLoop, calls=%fused_computation.7 | loop fusion | flops 7864320 | bytes 10485760 | tf_op jit(solution)/shard_map/reduce_sum | solution.py:177
  668.7 2.7 fusion.15
  (62 shorter events, 8.5 us)
Async XLA Ops:
  0.6 43.0 %copy-start = (bf16[1,128,4096]{2,1,0:T(8,128)(2,1)S(1)}, bf16[1,128,4096]{2,1,0:T(8,128)(2,1)}, u32[]{:S(2)}) copy-start(bf16[1,128,4096]{2,1,0:T(8,128)(2,1)} %param.10) | copy-start | bytes 3145732
  23.5 224.6 %all-to-all-start.1 = ((bf16[128,1,16,4096]{3,2,1,0:T(8,128)(2,1)}), bf16[128,1,16,4096]{3,2,1,0:T(8,128)(2,1)}, u32[]{:S(2)}, u32[]{:S(2)}) async-start(bf16[128,1,16,4096]{3,2,1,0:T(8,128)(2,1)} %bitcast.94), calls=%async_computation.1 | async-start | bytes 33554432 | tf_op jit(solution)/shard_map/all_to_all | solution.py:136
  33.9 9.6 %copy-start.3 = (s32[1,128,8]{1,2,0:T(8,128)S(1)}, s32[1,128,8]{1,2,0:T(8,128)}, u32[]{:S(2)}) copy-start(s32[1,128,8]{1,2,0:T(8,128)} %param.18) | copy-start | bytes 12292
  33.9 9.8 %copy-start.2 = (bf16[4096,128]{1,0:T(8,128)(2,1)S(1)}, bf16[4096,128]{1,0:T(8,128)(2,1)}, u32[]{:S(2)}) copy-start(bf16[4096,128]{1,0:T(8,128)(2,1)} %param.12) | copy-start | bytes 3145732
  248.0 38.4 %all-to-all-start = ((bf16[128,1,16]{2,1,0:T(2,128)(2,1)}), bf16[128,1,16]{2,1,0:T(2,128)(2,1)S(1)}, u32[]{:S(2)}, u32[]{:S(2)}) async-start(bf16[128,1,16]{2,1,0:T(2,128)(2,1)} %reshape.251), calls=%async_computation | async-start | bytes 131072 | tf_op jit(solution)/shard_map/all_to_all | solution.py:143
  286.4 14.9 %all-to-all-start.3 = ((bf16[1,128,16]{2,0,1:T(2,128)(2,1)}), bf16[1,128,16]{2,0,1:T(2,128)(2,1)S(1)}, u32[]{:S(2)}, u32[]{:S(2)}) async-start(bf16[1,128,16]{2,0,1:T(2,128)(2,1)} %convert_element_type.124), calls=%async_computation.3 | async-start | bytes 131072 | tf_op jit(solution)/shard_map/all_to_all | solution.py:168
  320.0 39.2 %all-to-all-start.5 = ((f32[64,32,128]{2,1,0:T(8,128)}), f32[64,32,128]{2,1,0:T(8,128)S(1)}, u32[]{:S(2)}, u32[]{:S(2)}) async-start(f32[64,32,128]{2,1,0:T(8,128)} %reduce_sum.111), calls=%async_computation.5 | async-start | bytes 2097152 | tf_op jit(solution)/shard_map/all_to_all | solution.py:32
  360.5 38.3 %all-to-all-start.6 = ((f32[64,32,128]{2,1,0:T(8,128)}), f32[64,32,128]{2,1,0:T(8,128)S(1)}, u32[]{:S(2)}, u32[]{:S(2)}) async-start(f32[64,32,128]{2,1,0:T(8,128)} %broadcast_in_dim.24), calls=%async_computation.6 | async-start | bytes 2097152 | tf_op jit(solution)/shard_map/all_to_all | solution.py:42
  404.4 232.1 %all-to-all-start.2 = ((bf16[1,128,16,4096]{3,2,0,1:T(8,128)(2,1)}), bf16[1,128,16,4096]{3,2,0,1:T(8,128)(2,1)}, u32[]{:S(2)}, u32[]{:S(2)}) async-start(bf16[1,128,16,4096]{3,2,0,1:T(8,128)(2,1)} %bitcast.95), calls=%async_computation.2 | async-start | bytes 33554432 | tf_op jit(solution)/shard_map/all_to_all | solution.py:161
  636.5 34.8 %copy-start.1 = (bf16[1,128,4096]{2,1,0:T(8,128)(2,1)S(1)}, bf16[1,128,4096]{2,1,0:T(8,128)(2,1)}, u32[]{:S(2)}) copy-start(bf16[1,128,4096]{2,1,0:T(8,128)(2,1)} %param.10) | copy-start | bytes 3145732
where the time goes:
time: 680 us; the launch traced here: 672 us
  waiting for transfers between devices  234 us (34%)
  blocking collectives  189 us (28%)
  matrix products  85.3 us (13%)
  local copies, waits for them, and re-layouts  82.7 us (12%)
  starting transfers between devices  66 us (10%)
  other arithmetic  13 us (2%)
    all_to_all x1, waiting for transfers between devices, shards(): lax.all_to_all(back_rows.reshape(1, devices, capacity, model_width), SEQ_...  220 us
    psum x2, blocking collectives, over_axes(): return functools.reduce(lax.psum, axes, shard)  178 us
    dot_general x1, matrix products, expert_backward(): jnp.einsum('rf,df->rd', grad_first, w_gate, preferred_element_type=jnp.fl...  29.5 us
    dot_general x1, matrix products, expert_backward(): jnp.einsum('rf,df->rd', grad_second, w_up, preferred_element_type=jnp.flo...  27.9 us
    gather x1, local copies, waits for them, and re-layouts, shards(): returned_rows[slot_index].reshape(tok_rows, top_count, model_width)  23.1 us
    dot_general x1, matrix products, expert_backward(): jnp.einsum('rd,fd->rf', grad_rows, w_down, preferred_element_type=jnp.flo...  22.5 us
    all_to_all x1, starting transfers between devices, shards(): lax.all_to_all(gate_slots.reshape(experts, 1, capacity), SEQ_EXP, split_a...  15.1 us
    gather x1, local copies, waits for them, and re-layouts, shards(): grad_slots = grad_padded[slot_token]  14.3 us
  transfers between devices with their start and end apart: 6, of which 3 were waited for; matrix products, arithmetic and copies ran while one was open for 16% of the time, Pallas kernels for 0%

commit v1 on v0

--- a/solution.py
+++ b/solution.py
@@ -140,12 +140,18 @@
             concat_axis=1,
             tiled=True,
         ),
-        lax.all_to_all(
-            gate_slots.reshape(experts, 1, capacity),
-            SEQ_EXP,
-            split_axis=0,
-            concat_axis=1,
-            tiled=True,
+        jnp.concatenate(
+            lax.all_to_all(
+                jnp.stack(
+                    jnp.split(
+                        gate_slots.reshape(experts, 1, capacity), lax.axis_size(SEQ_EXP), axis=0
+                    )
+                ),
+                SEQ_EXP,
+                0,
+                0,
+            ),
+            axis=1,
         ),
     )
     back_rows, slot_combine = expert_backward(

time: 680 us -> 782 us (1.15)
  local copies, waits for them, and re-layouts: 82.7 us -> 155 us
  blocking collectives: 189 us -> 208 us
  starting transfers between devices: 66 us -> 84.7 us
  waiting for transfers between devices: 234 us -> 225 us
    unnamed x12 -> x139, local copies, waits for them, and re-layouts: 11.1 us -> 83.9 us
    psum x2, blocking collectives: 178 us -> 197 us  [over_axes(): return functools.reduce(lax.psum, axes, shard)]
    all_to_all x1, starting transfers between devices: 9.72 us -> 19.8 us  [summed_rows(): return jnp.sum(lax.all_to_all(own, far, 0, 0, tiled=True), axis=0)]
    all_to_all x1, waiting for transfers between devices: 8.85 us -> 0.01 us  [shards(): lax.all_to_all(grad_slots.reshape(experts, 1, capacity, model_width), SEQ...]
    all_to_all x1, starting transfers between devices: 15.1 us -> 23.7 us  [shards(): lax.all_to_all(jnp.stack(jnp.split(gate_slots.reshape(experts, 1, capacit...]
  transfers between devices with their start and end apart: 6 -> 6, of which waited for: 3 -> 2; matrix products, arithmetic and copies ran while one was open for 16% -> 23% of each run, Pallas kernels for 0% -> 0%
where the time goes in v1:
time: 782 us; the launch traced here: 773 us
  waiting for transfers between devices  225 us (29%)
  blocking collectives  208 us (27%)
  local copies, waits for them, and re-layouts  155 us (20%)
  matrix products  85.3 us (11%)
  starting transfers between devices  84.7 us (11%)
  other arithmetic  13 us (2%)
    all_to_all x1, waiting for transfers between devices, shards(): lax.all_to_all(back_rows.reshape(1, devices, capacity, model_width), SEQ_...  220 us
    psum x2, blocking collectives, over_axes(): return functools.reduce(lax.psum, axes, shard)  197 us
    unnamed x139, local copies, waits for them, and re-layouts  83.9 us
    dot_general x1, matrix products, expert_backward(): jnp.einsum('rf,df->rd', grad_first, w_gate, preferred_element_type=jnp.fl...  29.5 us
    dot_general x1, matrix products, expert_backward(): jnp.einsum('rf,df->rd', grad_second, w_up, preferred_element_type=jnp.flo...  27.9 us
    all_to_all x1, starting transfers between devices, shards(): lax.all_to_all(jnp.stack(jnp.split(gate_slots.reshape(experts, 1, capacit...  23.7 us
    gather x1, local copies, waits for them, and re-layouts, shards(): returned_rows[slot_index].reshape(tok_rows, top_count, model_width)  23.1 us
    dot_general x1, matrix products, expert_backward(): jnp.einsum('rd,fd->rf', grad_rows, w_down, preferred_element_type=jnp.flo...  22.5 us
  transfers between devices with their start and end apart: 6, of which 2 were waited for; matrix products, arithmetic and copies ran while one was open for 23% of the time, Pallas kernels for 0%

profile of v1, /device:TPU:82, one launch (start us, length us, event | category | flops | bytes accessed | tf_op | source)
XLA Modules:
  0.0 773.0 jit_solution(10596206787214913176)
XLA Ops:
  0.6 0.9 copy.462
  3.5 4.3 scatter_custom_fusion.1
  7.8 1.3 concatenate.3
  9.2 14.3 %gather_fusion = bf16[2048,4096]{1,0:T(8,128)(2,1)} fusion(bf16[129,4096]{1,0:T(8,128)(2,1)S(1)} %concatenate.3, s32[2048]{0:T(1024)S(1)} %fusion.34), kind=kCustom, calls=%fused_computation | custom fusion | bytes 33562624 | tf_op jit(solution)/shard_map/gather | solution.py:126
  23.5 10.4 %all-to-all-start.1 = ((bf16[128,1,16,4096]{3,2,1,0:T(8,128)(2,1)}), bf16[128,1,16,4096]{3,2,1,0:T(8,128)(2,1)}, u32[]{:S(2)}, u32[]{:S(2)}) async-start(bf16[128,1,16,4096]{3,2,1,0:T(8,128)(2,1)} %bitcast.606), calls=%async_computation.1 | async-start | bytes 33554432 | tf_op jit(solution)/shard_map/all_to_all | solution.py:136
  34.7 7.0 gather_fusion.3
  42.2 134.7 %psum.14 = f32[128]{0:T(128)S(1)} all-reduce(f32[128]{0:T(128)S(1)} %convert_reduce_fusion.3), channel_id=1, replica_groups=mesh['seq_0'=4,'seq_1'=4,'exp_0'=4,'exp_1'=2] {'seq_0'}, use_global_device_ids=true, to_apply=%region_13.14 | all-reduce | flops 128 | bytes 1024 | tf_op jit(solution)/shard_map/psum | solution.py:14
  177.0 62.2 %psum.15 = f32[128]{0:T(128)S(1)} all-reduce(f32[128]{0:T(128)S(1)} %psum.14), channel_id=1, replica_groups=mesh['seq_0'=4,'seq_1'=4,'exp_0'=4,'exp_1'=2] {'seq_1'}, use_global_device_ids=true, to_apply=%region_14.15 | all-reduce | flops 128 | bytes 1024 | tf_op jit(solution)/shard_map/psum | solution.py:14
  240.0 7.6 scatter_custom_fusion
  279.2 4.7 copy.470
  283.9 4.7 copy.469
  330.6 23.7 %all-to-all-start = ((bf16[128,1,1,16]{3,2,1,0:T(2,128)(2,1)}), bf16[128,1,1,16]{3,2,1,0:T(2,128)(2,1)S(1)}, u32[]{:S(2)}, u32[]{:S(2)}) async-start(bf16[128,1,1,16]{3,2,1,0:T(2,128)(2,1)} %constant_dynamic-update-slice_fusion), calls=%async_computation | async-start | bytes 131072 | tf_op jit(solution)/shard_map/all_to_all | solution.py:144
  354.4 22.5 %fusion.4 = (bf16[2048]{0:T(1024)(128)(2,1)S(1)}, f32[2048,768]{0,1:T(8,128)}) fusion(bf16[1,2048,768]{1,2,0:T(8,128)(2,1)} %copy.469, bf16[1,2048,768]{1,2,0:T(8,128)(2,1)} %copy.470, bf16[2048,4096]{1,0:T(8,128)(2,1)} %bitcast.139, bf16[1,768,4096]{2,1,0:T(8,128)(2,1)} %param.15), kind=kOutput, calls=%fused_computation.17 | convolution fusion | flops 12899055616 | bytes 35655680 | tf_op jit(solution)/shard_map/rd,fd->rf/dot_general | solution.py:67
  376.9 0.7 convert_element_type.124
  377.6 9.8 %all-to-all-start.3 = ((bf16[1,128,16]{2,0,1:T(2,128)(2,1)}), bf16[1,128,16]{2,0,1:T(2,128)(2,1)S(1)}, u32[]{:S(2)}, u32[]{:S(2)}) async-start(bf16[1,128,16]{2,0,1:T(2,128)(2,1)} %convert_element_type.124), calls=%async_computation.3 | async-start | bytes 131072 | tf_op jit(solution)/shard_map/all_to_all | solution.py:174
  387.7 4.9 all-to-all-done.3
  392.8 6.8 gather_fusion.2
  400.7 1.8 convolution_bitcast_fusion
  402.5 1.9 copy.473
  404.6 5.4 all_to_all.52
  410.0 1.2 reduce_sum.111
  411.2 19.8 %all-to-all-start.5 = ((f32[64,32,128]{2,1,0:T(8,128)}), f32[64,32,128]{2,1,0:T(8,128)S(1)}, u32[]{:S(2)}, u32[]{:S(2)}) async-start(f32[64,32,128]{2,1,0:T(8,128)} %reduce_sum.111), calls=%async_computation.5 | async-start | bytes 2097152 | tf_op jit(solution)/shard_map/all_to_all | solution.py:32
  431.1 29.5 %fusion.10 = f32[2048,4096]{1,0:T(8,128)} fusion(bf16[1,4096,768]{2,1,0:T(8,128)(2,1)} %param.13, f32[2048,768]{0,1:T(8,128)} %get-tuple-element.21, bf16[1,2048,768]{1,2,0:T(8,128)(2,1)} %copy.469, bf16[1,2048,768]{1,2,0:T(8,128)(2,1)} %copy.470, f32[2048]{0:T(1024)S(1)} %reshape.443), kind=kOutput, calls=%fused_computation.23 | convolution fusion | flops 12905349120 | bytes 52436992 | tf_op jit(solution)/shard_map/rf,df->rd/dot_general | solution.py:79
  460.7 1.1 broadcast_in_dim.24
  461.8 10.3 %all-to-all-start.6 = ((f32[64,32,128]{2,1,0:T(8,128)}), f32[64,32,128]{2,1,0:T(8,128)S(1)}, u32[]{:S(2)}, u32[]{:S(2)}) async-start(f32[64,32,128]{2,1,0:T(8,128)} %broadcast_in_dim.24), calls=%async_computation.6 | async-start | bytes 2097152 | tf_op jit(solution)/shard_map/all_to_all | solution.py:42
  472.1 27.9 %add_convert_fusion = bf16[2048,4096]{1,0:T(8,128)(2,1)} fusion(f32[2048,4096]{1,0:T(8,128)} %fusion.10, bf16[1,4096,768]{2,1,0:T(8,128)(2,1)} %param.14, f32[2048,768]{0,1:T(8,128)} %get-tuple-element.21, f32[2048]{0:T(1024)S(1)} %reshape.443, bf16[1,2048,768]{1,2,0:T(8,128)(2,1)} %copy.470), kind=kOutput, calls=%fused_computation.6 | convolution fusion | flops 12914262016 | bytes 66068480 | tf_op jit(solution)/shard_map/rf,df->rd/dot_general | solution.py:80
  500.3 5.4 all_to_all.53
  505.7 10.6 %all-to-all-start.2 = ((bf16[1,128,16,4096]{3,2,0,1:T(8,128)(2,1)}), bf16[1,128,16,4096]{3,2,0,1:T(8,128)(2,1)}, u32[]{:S(2)}, u32[]{:S(2)}) async-start(bf16[1,128,16,4096]{3,2,0,1:T(8,128)(2,1)} %bitcast.607), calls=%async_computation.2 | async-start | bytes 33554432 | tf_op jit(solution)/shard_map/all_to_all | solution.py:167
  517.9 219.9 %all-to-all-done.2 = bf16[1,128,16,4096]{3,2,0,1:T(8,128)(2,1)} async-done(((bf16[1,128,16,4096]{3,2,0,1:T(8,128)(2,1)}), bf16[1,128,16,4096]{3,2,0,1:T(8,128)(2,1)}, u32[]{:S(2)}, u32[]{:S(2)}) %all-to-all-start.2) | async-done | bytes 16777248 | tf_op jit(solution)/shard_map/all_to_all | solution.py:167
  737.9 23.1 %gather_fusion.1 = bf16[1024,4096]{1,0:T(8,128)(2,1)} fusion(bf16[2048,4096]{1,0:T(8,128)(2,1)} %bitcast.148, s32[1024]{0:T(1024)S(1)} %broadcast_clamp_fusion), kind=kCustom, calls=%fused_computation.1 | custom fusion | bytes 16781312 | tf_op jit(solution)/shard_map/gather | solution.py:184
  760.9 9.1 %convert_reduce_fusion = f32[128,4096]{1,0:T(8,128)S(1)} fusion(bf16[1024,4096]{1,0:T(8,128)(2,1)} %gather_fusion.1), kind=kLoop, calls=%fused_computation.7 | loop fusion | flops 7864320 | bytes 10485760 | tf_op jit(solution)/shard_map/reduce_sum | solution.py:183
  770.0 2.7 fusion.15
  (189 shorter events, 80.5 us)
Async XLA Ops:
  0.6 33.3 %copy-start = (bf16[1,128,4096]{2,1,0:T(8,128)(2,1)S(1)}, bf16[1,128,4096]{2,1,0:T(8,128)(2,1)}, u32[]{:S(2)}) copy-start(bf16[1,128,4096]{2,1,0:T(8,128)(2,1)} %param.10) | copy-start | bytes 3145732
  23.5 10.4 %copy-start.3 = (s32[1,128,8]{1,2,0:T(8,128)S(1)}, s32[1,128,8]{1,2,0:T(8,128)}, u32[]{:S(2)}) copy-start(s32[1,128,8]{1,2,0:T(8,128)} %param.18) | copy-start | bytes 12292
  23.5 10.4 %copy-start.2 = (bf16[4096,128]{1,0:T(8,128)(2,1)S(1)}, bf16[4096,128]{1,0:T(8,128)(2,1)}, u32[]{:S(2)}) copy-start(bf16[4096,128]{1,0:T(8,128)(2,1)} %param.12) | copy-start | bytes 3145732
  23.5 307.1 %all-to-all-start.1 = ((bf16[128,1,16,4096]{3,2,1,0:T(8,128)(2,1)}), bf16[128,1,16,4096]{3,2,1,0:T(8,128)(2,1)}, u32[]{:S(2)}, u32[]{:S(2)}) async-start(bf16[128,1,16,4096]{3,2,1,0:T(8,128)(2,1)} %bitcast.606), calls=%async_computation.1 | async-start | bytes 33554432 | tf_op jit(solution)/shard_map/all_to_all | solution.py:136
  330.6 47.0 %all-to-all-start = ((bf16[128,1,1,16]{3,2,1,0:T(2,128)(2,1)}), bf16[128,1,1,16]{3,2,1,0:T(2,128)(2,1)S(1)}, u32[]{:S(2)}, u32[]{:S(2)}) async-start(bf16[128,1,1,16]{3,2,1,0:T(2,128)(2,1)} %constant_dynamic-update-slice_fusion), calls=%async_computation | async-start | bytes 131072 | tf_op jit(solution)/shard_map/all_to_all | solution.py:144
  377.6 14.9 %all-to-all-start.3 = ((bf16[1,128,16]{2,0,1:T(2,128)(2,1)}), bf16[1,128,16]{2,0,1:T(2,128)(2,1)S(1)}, u32[]{:S(2)}, u32[]{:S(2)}) async-start(bf16[1,128,16]{2,0,1:T(2,128)(2,1)} %convert_element_type.124), calls=%async_computation.3 | async-start | bytes 131072 | tf_op jit(solution)/shard_map/all_to_all | solution.py:174
  411.2 49.4 %all-to-all-start.5 = ((f32[64,32,128]{2,1,0:T(8,128)}), f32[64,32,128]{2,1,0:T(8,128)S(1)}, u32[]{:S(2)}, u32[]{:S(2)}) async-start(f32[64,32,128]{2,1,0:T(8,128)} %reduce_sum.111), calls=%async_computation.5 | async-start | bytes 2097152 | tf_op jit(solution)/shard_map/all_to_all | solution.py:32
  461.8 38.3 %all-to-all-start.6 = ((f32[64,32,128]{2,1,0:T(8,128)}), f32[64,32,128]{2,1,0:T(8,128)S(1)}, u32[]{:S(2)}, u32[]{:S(2)}) async-start(f32[64,32,128]{2,1,0:T(8,128)} %broadcast_in_dim.24), calls=%async_computation.6 | async-start | bytes 2097152 | tf_op jit(solution)/shard_map/all_to_all | solution.py:42
  505.7 232.1 %all-to-all-start.2 = ((bf16[1,128,16,4096]{3,2,0,1:T(8,128)(2,1)}), bf16[1,128,16,4096]{3,2,0,1:T(8,128)(2,1)}, u32[]{:S(2)}, u32[]{:S(2)}) async-start(bf16[1,128,16,4096]{3,2,0,1:T(8,128)(2,1)} %bitcast.607), calls=%async_computation.2 | async-start | bytes 33554432 | tf_op jit(solution)/shard_map/all_to_all | solution.py:167
  737.9 34.8 %copy-start.1 = (bf16[1,128,4096]{2,1,0:T(8,128)(2,1)S(1)}, bf16[1,128,4096]{2,1,0:T(8,128)(2,1)}, u32[]{:S(2)}) copy-start(bf16[1,128,4096]{2,1,0:T(8,128)(2,1)} %param.10) | copy-start | bytes 3145732
